TPU v7x, 32 devices: a whole 2x2x4 slice. The times are simulated.
32 devices in a mesh: rep: 4 (over y, core), row: 4 (over z), col: 2 (over x).
Axes of the slice: x: 2, y: 2, z: 4, core: 2. Of those that a mesh axis runs over, the one named last changes fastest.
Arguments:
- patches: bfloat16 [4096, 588], P(('rep', 'col')), may hold values from -20 to 20
- embed_weight: bfloat16 [588, 6144], P(None, 'row'), may hold values from -1 to 1
- embed_bias: float32 [6144], P('row'), may hold values from -3 to 3
- old_in: bfloat16 [64, 768, 1536], P(('row', 'col')), may hold values from -0.078125 to 0.078125
- old_out: bfloat16 [64, 1536, 768], P(('row', 'col')), may hold values from -0.0546875 to 0.0546875
- restore_id: int32 [1], replicated, may hold values from 0 to 47
- norm_gains: float32 [48, 6144], P(None, 'row'), may hold values from 0.1 to 1.9
- in_biases: float32 [48, 12288], P(None, 'col'), may hold values from -3 to 3
- out_biases: float32 [48, 6144], P(None, 'row'), may hold values from -3 to 3
- final_gain: float32 [6144], P('row'), may hold values from 0.1 to 1.9
- check_weight: bfloat16 [6144, 128], P('row'), may hold values from -0.078125 to 0.078125
Outputs:
- in_weight: bfloat16 [6144, 12288], P('row', 'col')
- out_weight: bfloat16 [12288, 6144], P('col', 'row')
- check_logits: float32 [4096, 128], P(('rep', 'col'))
All inputs are finite; a program needn't handle non-finite values.
Results may differ from a plain program's by a relative error of at most 0.0062.
Values may be sent and summed in bfloat16 or wider, within the bound.
A program may use at most 192 MiB of HBM per device.

v0:
```python
import jax
import jax.numpy as jnp
from jax import lax
from jax.sharding import PartitionSpec as P

EPSILON = 1e-06


def for_sending(shard):
    return jax.tree.map(lambda a: a.astype(jnp.bfloat16) if a.dtype == jnp.float32 else a, shard)


def partner(value, axis, bit):
    mask = 2**bit
    pairs = [(source, source ^ mask) for source in range(lax.axis_size(axis))]
    return lax.ppermute(value, axis, pairs)


def pick_rows(restore_id, param_table):
    selector = (
        jnp.arange(param_table.shape[0], dtype=jnp.int32)[None, :] == restore_id[:, None]
    ).astype(jnp.float32)
    return jnp.dot(selector, param_table, precision=lax.Precision.HIGHEST)[0]


def norm_rows(values, gain_row):
    feature_count = values.shape[1] * lax.axis_size("row")
    totals = lax.psum((jnp.sum(values, axis=1), jnp.sum(values * values, axis=1)), "row")
    average = totals[0][:, None] / feature_count
    spread = totals[1][:, None] / feature_count - average * average
    return ((values - average) * lax.rsqrt(spread + EPSILON) * gain_row).astype(jnp.bfloat16)


def move_halves(pieces, bit_total, device_index, exchange):
    for bit_number in range(bit_total):
        upper_side = device_index >> bit_number & 1 == 1
        outgoing = tuple(
            (jnp.where(upper_side, lower_part, upper_part) for lower_part, upper_part in pieces)
        )
        incoming = exchange(outgoing, bit_number)
        pieces = tuple(
            (
                (
                    jnp.where(upper_side, arrived, lower_part),
                    jnp.where(upper_side, upper_part, arrived),
                )
                for (lower_part, upper_part), arrived in zip(pieces, incoming)
            )
        )
    return pieces


def on_device(
    patches,
    embed_weight,
    embed_bias,
    old_in,
    old_out,
    restore_id,
    norm_gains,
    in_biases,
    out_biases,
    final_gain,
    check_weight,
):
    tiles_here, tile_rows, tile_cols = old_in.shape
    local_cols = tiles_here * tile_cols
    half_cols = local_cols // 2
    in_local = jnp.transpose(old_in, (1, 0, 2)).reshape(tile_rows, local_cols)
    out_local = old_out.reshape(local_cols, tile_rows)
    col_index = lax.axis_index("col")
    col_count = lax.axis_size("col")
    col_bits = col_count.bit_length() - 1
    pieces = (
        (in_local[:, :half_cols], in_local[:, half_cols:]),
        (out_local[:half_cols], out_local[half_cols:]),
    )
    pieces = move_halves(
        pieces,
        col_bits,
        col_index,
        lambda send_parts, bit_number: jax.tree.map(
            lambda part, own: part.astype(own.dtype),
            partner(for_sending(send_parts), "col", bit_number),
            send_parts,
        ),
    )
    in_pair, out_pair = pieces
    in_weight = jnp.concatenate(in_pair, axis=0)
    out_weight = jnp.concatenate(out_pair, axis=1)
    layer_gain = pick_rows(restore_id, norm_gains)
    in_bias = pick_rows(restore_id, in_biases)
    out_bias = pick_rows(restore_id, out_biases)
    embedded = jnp.dot(patches, embed_weight, preferred_element_type=jnp.float32) + embed_bias
    normed = norm_rows(embedded, layer_gain)
    partial_pre = jnp.dot(
        lax.all_gather(normed, "col", axis=0, tiled=True),
        in_weight,
        preferred_element_type=jnp.float32,
    )
    pre_share = lax.psum_scatter(partial_pre, "row", scatter_dimension=0, tiled=True) + in_bias
    hidden = jax.nn.gelu(pre_share, approximate=False).astype(jnp.bfloat16)
    partial_branch = jnp.dot(
        lax.all_gather(hidden, "row", axis=0, tiled=True),
        out_weight,
        preferred_element_type=jnp.float32,
    )
    updated = (
        embedded
        + lax.psum_scatter(partial_branch, "col", scatter_dimension=0, tiled=True)
        + out_bias
    )
    final_normed = norm_rows(updated, final_gain)
    check_logits = lax.psum(
        jnp.dot(final_normed, check_weight, preferred_element_type=jnp.float32), "row"
    )
    return (in_weight, out_weight, check_logits)


def solution(mesh):
    placed = (
        P(("rep", "col"), None),
        P(None, "row"),
        P("row"),
        P(("row", "col"), None, None),
        P(("row", "col"), None, None),
        P(),
        P(None, "row"),
        P(None, "col"),
        P(None, "row"),
        P("row"),
        P("row", None),
    )
    return jax.shard_map(
        on_device,
        mesh=mesh,
        in_specs=placed,
        out_specs=(P("row", "col"), P("col", "row"), P(("rep", "col"), None)),
        check_vma=False,
    )
```

profile of v0, /device:TPU:0, one launch (start us, length us, event | category | flops | bytes accessed | tf_op | source)
XLA Modules:
  0.0 1160.1 jit_solution(9391864358575194546)
XLA Ops:
  7.2 0.0 copy-start
  7.2 0.0 all-gather.3.cloned.1.call-start
  7.2 10.0 copy.15
  17.2 0.0 copy-start.2
  17.2 0.0 copy-start.8
  17.2 0.0 copy-start.9
  17.2 4.0 broadcast_select_fusion.2
  21.3 5.6 copy-done.2
  26.9 0.0 copy-start.5
  26.9 3.0 collective-permute-start
  30.5 0.0 copy-done
  30.5 0.0 copy-done.8
  30.5 0.0 copy-done.9
  30.5 3.2 fusion.22
  33.7 11.9 %all-reduce.1 = (f32[512]{0:T(512)S(1)}, f32[512]{0:T(512)S(1)}) all-reduce(f32[512]{0:T(512)S(1)} %get-tuple-element.6, f32[512]{0:T(512)S(1)} %get-tuple-element.5), channel_id=1, replica_groups=mesh['rep'=4,'row'=4,'col'=2] {'row'}, use_global_device_ids=true, to_apply=%region_3.4 | all-reduce | flops 1024 | bytes 8192 | tf_op jit(solution)/shard_map/psum | solution.py:28
  45.7 0.0 copy-done.5
  45.7 0.2 convolution_reduce_fusion.1
  45.9 3.6 multiply_convert_fusion.1
  49.5 0.0 all-gather.3.cloned.1.call-update
  49.5 0.0 reduce-scatter.3.cloned.1.call-start
  49.6 217.2 %collective-permute-done = bf16[768,6144]{1,0:T(8,128)(2,1)} collective-permute-done((bf16[768,6144]{1,0:T(8,128)(2,1)}, bf16[768,6144]{1,0:T(8,128)(2,1)}, u32[]{:S(2)}, u32[]{:S(2)}) %collective-permute-start) | collective-permute-done | bytes 9437216 | tf_op jit(solution)/shard_map/ppermute | solution.py:16
  266.8 9.7 broadcast_select_fusion.1
  276.5 21.6 %pad_maximum_fusion = bf16[1536,6144]{1,0:T(8,128)(2,1)} fusion(bf16[768,6144]{1,0:T(8,128)(2,1)S(1)} %get-tuple-element.13, bf16[768,6144]{1,0:T(8,128)(2,1)S(1)} %get-tuple-element.12), kind=kLoop, calls=%fused_computation | loop fusion | flops 37748736 | bytes 37748736 | tf_op jit(solution)/shard_map/concatenate | solution.py:89
  298.1 0.0 all-gather.3.cloned.1.call-done
  298.1 26.1 %fusion.24 = f32[1024,6144]{1,0:T(8,128)} fusion(bf16[1024,1536]{1,0:T(8,128)(2,1)} %all-gather.3.cloned.1.call-done, bf16[1536,6144]{1,0:T(8,128)(2,1)} %pad_maximum_fusion), kind=kOutput, calls=%fused_computation.54 | convolution fusion | flops 19327352832 | bytes 47185920 | tf_op jit(solution)/shard_map/dot_general | solution.py:96
  324.3 0.0 copy-start.3
  324.3 0.0 reduce-scatter.3.cloned.1.call-update
  324.3 0.0 all-gather.5.cloned.1.call-start
  324.3 1.2 copy-done.3
  325.5 0.5 fusion.15
  326.0 414.1 %reduce-scatter.3.cloned.1.call-done = f32[256,6144]{1,0:T(8,128)} async-done(((f32[1024,6144]{1,0:T(8,128)}), f32[256,6144]{1,0:T(8,128)}) %reduce-scatter.3.cloned.1.call-update) | async-done | bytes 6291472 | tf_op jit(solution)/shard_map/reduce_scatter | solution.py:101
  740.1 15.9 %fusion.2 = bf16[256,6144]{1,0:T(8,128)(2,1)} fusion(f32[256,6144]{1,0:T(8,128)} %reduce-scatter.3.cloned.1.call-done, f32[6144]{0:T(1024)S(1)} %bitcast.36), kind=kLoop, calls=%fused_computation.11 | loop fusion | flops 103809024 | bytes 9461760 | tf_op jit(solution)/shard_map/convert_element_type | solution.py:102
  756.0 0.0 all-gather.5.cloned.1.call-update
  756.0 0.2 reduce-scatter.5.cloned.1.call-start
  756.3 7.5 fusion.23
  763.8 1.1 bitcast_select_fusion.1
  764.8 1.5 collective-permute-start.1
  766.4 203.3 %collective-permute-done.1 = bf16[6144,768]{1,0:T(8,128)(2,1)} collective-permute-done((bf16[6144,768]{1,0:T(8,128)(2,1)S(1)}, bf16[6144,768]{1,0:T(8,128)(2,1)}, u32[]{:S(2)}, u32[]{:S(2)}) %collective-permute-start.1) | collective-permute-done | bytes 9437216 | tf_op jit(solution)/shard_map/ppermute | solution.py:16
  969.7 9.6 bitcast_select_fusion.2
  979.3 14.5 %pad_maximum_fusion.1 = bf16[6144,1536]{1,0:T(8,128)(2,1)} fusion(bf16[6144,768]{1,0:T(8,128)(2,1)} %get-tuple-element.17, bf16[6144,768]{1,0:T(8,128)(2,1)S(1)} %get-tuple-element.16), kind=kLoop, calls=%fused_computation.1 | loop fusion | flops 37748736 | bytes 37748736 | tf_op jit(solution)/shard_map/concatenate | solution.py:90
  993.8 0.0 all-gather.5.cloned.1.call-done
  993.8 26.1 %fusion.25 = f32[1024,1536]{1,0:T(8,128)} fusion(bf16[1024,6144]{1,0:T(8,128)(2,1)} %all-gather.5.cloned.1.call-done, bf16[6144,1536]{1,0:T(8,128)(2,1)} %pad_maximum_fusion.1), kind=kOutput, calls=%fused_computation.55 | convolution fusion | flops 19327352832 | bytes 37748736 | tf_op jit(solution)/shard_map/dot_general | solution.py:103
  1019.9 0.0 copy-start.6
  1019.9 0.0 reduce-scatter.5.cloned.1.call-update
  1020.0 0.0 copy-start.4
  1020.0 0.0 copy-start.7
  1020.0 0.0 all-reduce.4.cloned.1.call-start
  1020.0 0.9 copy-done.6
  1020.9 0.0 copy-start.1
  1020.9 0.2 convolution_reduce_fusion
  1021.1 78.1 %reduce-scatter.5.cloned.1.call-done = f32[512,1536]{1,0:T(8,128)} async-done(((f32[1024,1536]{1,0:T(8,128)}), f32[512,1536]{1,0:T(8,128)}) %reduce-scatter.5.cloned.1.call-update) | async-done | bytes 3145744 | tf_op jit(solution)/shard_map/reduce_scatter | solution.py:110
  1099.2 4.8 fusion.21
  1104.0 11.7 %all-reduce = (f32[512]{0:T(512)S(1)}, f32[512]{0:T(512)S(1)}) all-reduce(f32[512]{0:T(512)S(1)} %get-tuple-element.4, f32[512]{0:T(512)S(1)} %get-tuple-element.3), channel_id=1, replica_groups=mesh['rep'=4,'row'=4,'col'=2] {'row'}, use_global_device_ids=true, to_apply=%region_9.10 | all-reduce | flops 1024 | bytes 8192 | tf_op jit(solution)/shard_map/psum | solution.py:28
  1115.7 0.0 copy-done.4
  1115.7 0.0 copy-done.7
  1115.7 3.2 fusion.10
  1118.9 0.0 all-reduce.4.cloned.1.call-update
  1119.0 33.0 %all-reduce.4.cloned.1.call-done = f32[512,128]{1,0:T(8,128)} async-done(((f32[512,128]{1,0:T(8,128)}), f32[512,128]{1,0:T(8,128)}) %all-reduce.4.cloned.1.call-update) | async-done | bytes 262160 | tf_op jit(solution)/shard_map/psum | solution.py:114
  1151.9 1.7 copy.18
  1153.6 0.0 copy-done.1
  (2 shorter events, 0.0 us)
Async XLA Ops:
  7.2 23.3 %copy-start = (bf16[588,1536]{1,0:T(8,128)(2,1)S(1)}, bf16[588,1536]{1,0:T(8,128)(2,1)}, u32[]{:S(2)}) copy-start(bf16[588,1536]{1,0:T(8,128)(2,1)} %param.12) | copy-start | bytes 5419012
  7.2 291.0 %all-gather.3.cloned.1.call-start = ((), (), s32[]{:S(2)}) async-start(), calls=%async_computation.2 | async-start | bytes 4718592 | tf_op jit(solution)/shard_map/all_gather | solution.py:97
  17.2 9.7 copy-start.2
  17.2 13.3 %copy-start.8 = (bf16[512,588]{0,1:T(8,128)(2,1)S(1)}, bf16[512,588]{0,1:T(8,128)(2,1)}, u32[]{:S(2)}) copy-start(bf16[512,588]{0,1:T(8,128)(2,1)} %param.11) | copy-start | bytes 1806340
  17.2 13.3 %copy-start.9 = (f32[1536]{0:T(1024)S(1)}, f32[1536]{0:T(1024)}, u32[]{:S(2)}) copy-start(f32[1536]{0:T(1024)} %param.13) | copy-start | bytes 18436
  26.9 18.8 %copy-start.5 = (f32[48,1536]{1,0:T(8,128)S(1)}, f32[48,1536]{1,0:T(8,128)}, u32[]{:S(2)}) copy-start(f32[48,1536]{1,0:T(8,128)} %param.17) | copy-start | bytes 884740
  26.9 239.9 %collective-permute-start = (bf16[768,6144]{1,0:T(8,128)(2,1)}, bf16[768,6144]{1,0:T(8,128)(2,1)}, u32[]{:S(2)}, u32[]{:S(2)}) collective-permute-start(bf16[768,6144]{1,0:T(8,128)(2,1)} %broadcast_select_fusion.2), channel_id=1, source_target_pairs={{0,1},{1,0},{2,3},{3,2},{4,5},{5,4},{6,7},{7,6},{8,9},{9,8},{10,11... | collective-permute-start | bytes 28311560 | tf_op jit(solution)/shard_map/ppermute | solution.py:16
  49.5 690.6 %reduce-scatter.3.cloned.1.call-start = ((), (), s32[]{:S(2)}) async-start(), calls=%async_computation.3 | async-start | bytes 31457280 | tf_op jit(solution)/shard_map/reduce_scatter | solution.py:101
  324.3 1.3 copy-start.3
  324.3 669.5 %all-gather.5.cloned.1.call-start = ((), (), s32[]{:S(2)}) async-start(), calls=%async_computation.4 | async-start | bytes 15728640 | tf_op jit(solution)/shard_map/all_gather | solution.py:104
  756.0 343.1 %reduce-scatter.5.cloned.1.call-start = ((), (), s32[]{:S(2)}) async-start(), calls=%async_computation.5 | async-start | bytes 9437184 | tf_op jit(solution)/shard_map/reduce_scatter | solution.py:110
  764.8 204.9 %collective-permute-start.1 = (bf16[6144,768]{1,0:T(8,128)(2,1)S(1)}, bf16[6144,768]{1,0:T(8,128)(2,1)}, u32[]{:S(2)}, u32[]{:S(2)}) collective-permute-start(bf16[6144,768]{1,0:T(8,128)(2,1)S(1)} %bitcast_select_fusion.1), channel_id=1, source_target_pairs={{0,1},{1,0},{2,3},{3,2},{4,5},{5,4},{6,7},{7,6},{8,9},{9,8},{10,11... | collective-permute-start | bytes 28311560 | tf_op jit(solution)/shard_map/ppermute | solution.py:16
  1019.9 1.0 copy-start.6
  1020.0 95.8 %copy-start.4 = (bf16[1536,128]{1,0:T(8,128)(2,1)S(1)}, bf16[1536,128]{1,0:T(8,128)(2,1)}, u32[]{:S(2)}) copy-start(bf16[1536,128]{1,0:T(8,128)(2,1)} %param.21) | copy-start | bytes 1179652
  1020.0 95.7 %copy-start.7 = (f32[1536]{0:T(1024)S(1)}, f32[1536]{0:T(1024)}, u32[]{:S(2)}) copy-start(f32[1536]{0:T(1024)} %param.20) | copy-start | bytes 18436
  1020.0 132.0 %all-reduce.4.cloned.1.call-start = ((), (), s32[]{:S(2)}) async-start(), calls=%async_computation.6 | async-start | bytes 524288 | tf_op jit(solution)/shard_map/psum | solution.py:114
  1020.9 132.7 %copy-start.1 = (bf16[588,1536]{1,0:T(8,128)(2,1)S(1)}, bf16[588,1536]{1,0:T(8,128)(2,1)}, u32[]{:S(2)}) copy-start(bf16[588,1536]{1,0:T(8,128)(2,1)} %param.12) | copy-start | bytes 5419012
Sparse Core Ops, SparseCore 0:
  49.6 75.9 all-gather.2
  324.4 415.6 reduce-scatter.2
  756.2 220.1 all-gather.4
  1020.1 79.0 reduce-scatter.4
  1119.1 32.8 all-reduce.3
where the time goes:
time: 1160 us
  waiting for transfers between devices  946 us (82%)
  other arithmetic  84.8 us (7%)
  matrix products  59.6 us (5%)
  local copies, waits for them, and re-layouts  26.9 us (2%)
  blocking collectives  23.6 us (2%)
  between operations  14.6 us (1%)
    ppermute x2, waiting for transfers between devices, partner(): return lax.ppermute(value, axis, pairs)  421 us
    reduce_scatter x1, waiting for transfers between devices, on_device(): lax.psum_scatter(partial_pre, 'row', scatter_dimension=0, tiled=True)  414 us
    reduce_scatter x1, waiting for transfers between devices, on_device(): lax.psum_scatter(partial_branch, 'col', scatter_dimension=0, tiled=True)  78.1 us
    psum x1, waiting for transfers between devices, on_device(): lax.psum(jnp.dot(final_normed, check_weight, preferred_element_type=jnp.f...  33 us
    dot_general x1, matrix products, on_device(): jnp.dot(lax.all_gather(hidden, 'row', axis=0, tiled=True), out_weight, pr...  26.1 us
    dot_general x1, matrix products, on_device(): jnp.dot(lax.all_gather(normed, 'col', axis=0, tiled=True), in_weight, pre...  26.1 us
    psum x2, blocking collectives, norm_rows(): lax.psum((jnp.sum(values, axis=1), jnp.sum(values * values, axis=1)), 'row')  23.6 us
  transfers between devices with their start and end apart: 7, of which 5 were waited for; matrix products, arithmetic and copies ran while one was open for 6% of the time, Pallas kernels for 0%

commit v1 on v0

--- a/solution.py
+++ b/solution.py
@@ -111,9 +111,9 @@
         + out_bias
     )
     final_normed = norm_rows(updated, final_gain)
-    check_logits = lax.psum(
-        jnp.dot(final_normed, check_weight, preferred_element_type=jnp.float32), "row"
-    )
+    x = jnp.dot(final_normed, check_weight, preferred_element_type=jnp.float32)
+    parts = lax.all_gather(x, "row", axis=0, tiled=False)
+    check_logits = parts.sum(axis=0)
     return (in_weight, out_weight, check_logits)
 
 

time: 1160 us -> 1150 us (level)
    psum x1 -> x0, waiting for transfers between devices: 33 us -> none  [on_device(): lax.psum(jnp.dot(final_normed, check_weight, preferred_element_type=jnp.f...]
    all_gather x0 -> x1, waiting for transfers between devices: none -> 25.4 us  [on_device(): parts = lax.all_gather(x, 'row', axis=0, tiled=False)]
where the time goes in v1:
time: 1150 us
  waiting for transfers between devices  938 us (82%)
  other arithmetic  86.8 us (8%)
  matrix products  59.6 us (5%)
  local copies, waits for them, and re-layouts  25.2 us (2%)
  blocking collectives  23.6 us (2%)
  between operations  14.6 us (1%)
    ppermute x2, waiting for transfers between devices, partner(): return lax.ppermute(value, axis, pairs)  421 us
    reduce_scatter x1, waiting for transfers between devices, on_device(): lax.psum_scatter(partial_pre, 'row', scatter_dimension=0, tiled=True)  414 us
    reduce_scatter x1, waiting for transfers between devices, on_device(): lax.psum_scatter(partial_branch, 'col', scatter_dimension=0, tiled=True)  78.1 us
    dot_general x1, matrix products, on_device(): jnp.dot(lax.all_gather(hidden, 'row', axis=0, tiled=True), out_weight, pr...  26.1 us
    dot_general x1, matrix products, on_device(): jnp.dot(lax.all_gather(normed, 'col', axis=0, tiled=True), in_weight, pre...  26.1 us
    all_gather x1, waiting for transfers between devices, on_device(): parts = lax.all_gather(x, 'row', axis=0, tiled=False)  25.4 us
    psum x2, blocking collectives, norm_rows(): lax.psum((jnp.sum(values, axis=1), jnp.sum(values * values, axis=1)), 'row')  23.6 us
  transfers between devices with their start and end apart: 7, of which 5 were waited for; matrix products, arithmetic and copies ran while one was open for 6% of the time, Pallas kernels for 0%

profile of v1, /device:TPU:0, one launch (start us, length us, event | category | flops | bytes accessed | tf_op | source)
XLA Modules:
  0.0 1152.9 jit_solution(8650716443930202391)
XLA Ops:
  7.2 0.0 copy-start
  7.2 0.0 all-gather.5.cloned.1.call-start
  7.2 10.0 copy.15
  17.2 0.0 copy-start.2
  17.2 0.0 copy-start.8
  17.2 0.0 copy-start.9
  17.2 4.0 broadcast_select_fusion.2
  21.3 5.6 copy-done.2
  26.9 0.0 copy-start.5
  26.9 3.0 collective-permute-start
  30.5 0.0 copy-done
  30.5 0.0 copy-done.8
  30.5 0.0 copy-done.9
  30.5 3.2 fusion.22
  33.7 11.9 %all-reduce.1 = (f32[512]{0:T(512)S(1)}, f32[512]{0:T(512)S(1)}) all-reduce(f32[512]{0:T(512)S(1)} %get-tuple-element.6, f32[512]{0:T(512)S(1)} %get-tuple-element.5), channel_id=1, replica_groups=mesh['rep'=4,'row'=4,'col'=2] {'row'}, use_global_device_ids=true, to_apply=%region_3.4 | all-reduce | flops 1024 | bytes 8192 | tf_op jit(solution)/shard_map/psum | solution.py:28
  45.7 0.0 copy-done.5
  45.7 0.2 convolution_reduce_fusion.1
  45.9 3.6 multiply_convert_fusion.1
  49.5 0.0 all-gather.5.cloned.1.call-update
  49.5 0.0 reduce-scatter.3.cloned.1.call-start
  49.6 217.2 %collective-permute-done = bf16[768,6144]{1,0:T(8,128)(2,1)} collective-permute-done((bf16[768,6144]{1,0:T(8,128)(2,1)}, bf16[768,6144]{1,0:T(8,128)(2,1)}, u32[]{:S(2)}, u32[]{:S(2)}) %collective-permute-start) | collective-permute-done | bytes 9437216 | tf_op jit(solution)/shard_map/ppermute | solution.py:16
  266.8 9.7 broadcast_select_fusion.1
  276.5 21.6 %pad_maximum_fusion = bf16[1536,6144]{1,0:T(8,128)(2,1)} fusion(bf16[768,6144]{1,0:T(8,128)(2,1)S(1)} %get-tuple-element.13, bf16[768,6144]{1,0:T(8,128)(2,1)S(1)} %get-tuple-element.12), kind=kLoop, calls=%fused_computation | loop fusion | flops 37748736 | bytes 37748736 | tf_op jit(solution)/shard_map/concatenate | solution.py:89
  298.1 0.0 all-gather.5.cloned.1.call-done
  298.1 26.1 %fusion.24 = f32[1024,6144]{1,0:T(8,128)} fusion(bf16[1024,1536]{1,0:T(8,128)(2,1)} %all-gather.5.cloned.1.call-done, bf16[1536,6144]{1,0:T(8,128)(2,1)} %pad_maximum_fusion), kind=kOutput, calls=%fused_computation.54 | convolution fusion | flops 19327352832 | bytes 47185920 | tf_op jit(solution)/shard_map/dot_general | solution.py:96
  324.3 0.0 copy-start.3
  324.3 0.0 reduce-scatter.3.cloned.1.call-update
  324.3 0.0 all-gather.7.cloned.1.call-start
  324.3 1.2 copy-done.3
  325.5 0.5 fusion.15
  326.0 414.1 %reduce-scatter.3.cloned.1.call-done = f32[256,6144]{1,0:T(8,128)} async-done(((f32[1024,6144]{1,0:T(8,128)}), f32[256,6144]{1,0:T(8,128)}) %reduce-scatter.3.cloned.1.call-update) | async-done | bytes 6291472 | tf_op jit(solution)/shard_map/reduce_scatter | solution.py:101
  740.1 15.9 %fusion.2 = bf16[256,6144]{1,0:T(8,128)(2,1)} fusion(f32[256,6144]{1,0:T(8,128)} %reduce-scatter.3.cloned.1.call-done, f32[6144]{0:T(1024)S(1)} %bitcast.38), kind=kLoop, calls=%fused_computation.11 | loop fusion | flops 103809024 | bytes 9461760 | tf_op jit(solution)/shard_map/convert_element_type | solution.py:102
  756.0 0.0 all-gather.7.cloned.1.call-update
  756.0 0.2 reduce-scatter.5.cloned.1.call-start
  756.3 7.5 fusion.23
  763.8 1.1 bitcast_select_fusion.1
  764.8 1.5 collective-permute-start.1
  766.4 203.3 %collective-permute-done.1 = bf16[6144,768]{1,0:T(8,128)(2,1)} collective-permute-done((bf16[6144,768]{1,0:T(8,128)(2,1)S(1)}, bf16[6144,768]{1,0:T(8,128)(2,1)}, u32[]{:S(2)}, u32[]{:S(2)}) %collective-permute-start.1) | collective-permute-done | bytes 9437216 | tf_op jit(solution)/shard_map/ppermute | solution.py:16
  969.7 9.6 bitcast_select_fusion.2
  979.3 14.5 %pad_maximum_fusion.1 = bf16[6144,1536]{1,0:T(8,128)(2,1)} fusion(bf16[6144,768]{1,0:T(8,128)(2,1)} %get-tuple-element.17, bf16[6144,768]{1,0:T(8,128)(2,1)S(1)} %get-tuple-element.16), kind=kLoop, calls=%fused_computation.1 | loop fusion | flops 37748736 | bytes 37748736 | tf_op jit(solution)/shard_map/concatenate | solution.py:90
  993.8 0.0 all-gather.7.cloned.1.call-done
  993.8 26.1 %fusion.25 = f32[1024,1536]{1,0:T(8,128)} fusion(bf16[1024,6144]{1,0:T(8,128)(2,1)} %all-gather.7.cloned.1.call-done, bf16[6144,1536]{1,0:T(8,128)(2,1)} %pad_maximum_fusion.1), kind=kOutput, calls=%fused_computation.55 | convolution fusion | flops 19327352832 | bytes 37748736 | tf_op jit(solution)/shard_map/dot_general | solution.py:103
  1019.9 0.0 copy-start.6
  1019.9 0.0 reduce-scatter.5.cloned.1.call-update
  1020.0 0.0 copy-start.4
  1020.0 0.0 copy-start.7
  1020.0 0.0 all-gather.9.cloned.1.call-start
  1020.0 0.9 copy-done.6
  1020.9 0.0 copy-start.1
  1020.9 0.2 convolution_reduce_fusion
  1021.1 78.1 %reduce-scatter.5.cloned.1.call-done = f32[512,1536]{1,0:T(8,128)} async-done(((f32[1024,1536]{1,0:T(8,128)}), f32[512,1536]{1,0:T(8,128)}) %reduce-scatter.5.cloned.1.call-update) | async-done | bytes 3145744 | tf_op jit(solution)/shard_map/reduce_scatter | solution.py:110
  1099.2 4.8 fusion.21
  1104.0 11.7 %all-reduce = (f32[512]{0:T(512)S(1)}, f32[512]{0:T(512)S(1)}) all-reduce(f32[512]{0:T(512)S(1)} %get-tuple-element.4, f32[512]{0:T(512)S(1)} %get-tuple-element.3), channel_id=1, replica_groups=mesh['rep'=4,'row'=4,'col'=2] {'row'}, use_global_device_ids=true, to_apply=%region_9.10 | all-reduce | flops 1024 | bytes 8192 | tf_op jit(solution)/shard_map/psum | solution.py:28
  1115.7 0.0 copy-done.4
  1115.7 0.0 copy-done.7
  1115.7 3.2 fusion.10
  1118.9 0.0 all-gather.9.cloned.1.call-update
  1119.0 25.4 %all-gather.9.cloned.1.call-done = f32[2048,128]{1,0:T(8,128)} async-done(((f32[512,128]{1,0:T(8,128)}), f32[2048,128]{1,0:T(8,128)}) %all-gather.9.cloned.1.call-update) | async-done | bytes 1048592 | tf_op jit(solution)/shard_map/all_gather | solution.py:115
  1144.3 2.0 reduce_sum.49
  1146.3 0.0 copy-done.1
  (2 shorter events, 0.0 us)
Async XLA Ops:
  7.2 23.3 %copy-start = (bf16[588,1536]{1,0:T(8,128)(2,1)S(1)}, bf16[588,1536]{1,0:T(8,128)(2,1)}, u32[]{:S(2)}) copy-start(bf16[588,1536]{1,0:T(8,128)(2,1)} %param.12) | copy-start | bytes 5419012
  7.2 291.0 %all-gather.5.cloned.1.call-start = ((), (), s32[]{:S(2)}) async-start(), calls=%async_computation.2 | async-start | bytes 4718592 | tf_op jit(solution)/shard_map/all_gather | solution.py:97
  17.2 9.7 copy-start.2
  17.2 13.3 %copy-start.8 = (bf16[512,588]{0,1:T(8,128)(2,1)S(1)}, bf16[512,588]{0,1:T(8,128)(2,1)}, u32[]{:S(2)}) copy-start(bf16[512,588]{0,1:T(8,128)(2,1)} %param.11) | copy-start | bytes 1806340
  17.2 13.3 %copy-start.9 = (f32[1536]{0:T(1024)S(1)}, f32[1536]{0:T(1024)}, u32[]{:S(2)}) copy-start(f32[1536]{0:T(1024)} %param.13) | copy-start | bytes 18436
  26.9 18.8 %copy-start.5 = (f32[48,1536]{1,0:T(8,128)S(1)}, f32[48,1536]{1,0:T(8,128)}, u32[]{:S(2)}) copy-start(f32[48,1536]{1,0:T(8,128)} %param.17) | copy-start | bytes 884740
  26.9 239.9 %collective-permute-start = (bf16[768,6144]{1,0:T(8,128)(2,1)}, bf16[768,6144]{1,0:T(8,128)(2,1)}, u32[]{:S(2)}, u32[]{:S(2)}) collective-permute-start(bf16[768,6144]{1,0:T(8,128)(2,1)} %broadcast_select_fusion.2), channel_id=1, source_target_pairs={{0,1},{1,0},{2,3},{3,2},{4,5},{5,4},{6,7},{7,6},{8,9},{9,8},{10,11... | collective-permute-start | bytes 28311560 | tf_op jit(solution)/shard_map/ppermute | solution.py:16
  49.5 690.6 %reduce-scatter.3.cloned.1.call-start = ((), (), s32[]{:S(2)}) async-start(), calls=%async_computation.3 | async-start | bytes 31457280 | tf_op jit(solution)/shard_map/reduce_scatter | solution.py:101
  324.3 1.3 copy-start.3
  324.3 669.5 %all-gather.7.cloned.1.call-start = ((), (), s32[]{:S(2)}) async-start(), calls=%async_computation.4 | async-start | bytes 15728640 | tf_op jit(solution)/shard_map/all_gather | solution.py:104
  756.0 343.1 %reduce-scatter.5.cloned.1.call-start = ((), (), s32[]{:S(2)}) async-start(), calls=%async_computation.5 | async-start | bytes 9437184 | tf_op jit(solution)/shard_map/reduce_scatter | solution.py:110
  764.8 204.9 %collective-permute-start.1 = (bf16[6144,768]{1,0:T(8,128)(2,1)S(1)}, bf16[6144,768]{1,0:T(8,128)(2,1)}, u32[]{:S(2)}, u32[]{:S(2)}) collective-permute-start(bf16[6144,768]{1,0:T(8,128)(2,1)S(1)} %bitcast_select_fusion.1), channel_id=1, source_target_pairs={{0,1},{1,0},{2,3},{3,2},{4,5},{5,4},{6,7},{7,6},{8,9},{9,8},{10,11... | collective-permute-start | bytes 28311560 | tf_op jit(solution)/shard_map/ppermute | solution.py:16
  1019.9 1.0 copy-start.6
  1020.0 95.8 %copy-start.4 = (bf16[1536,128]{1,0:T(8,128)(2,1)S(1)}, bf16[1536,128]{1,0:T(8,128)(2,1)}, u32[]{:S(2)}) copy-start(bf16[1536,128]{1,0:T(8,128)(2,1)} %param.21) | copy-start | bytes 1179652
  1020.0 95.7 %copy-start.7 = (f32[1536]{0:T(1024)S(1)}, f32[1536]{0:T(1024)}, u32[]{:S(2)}) copy-start(f32[1536]{0:T(1024)} %param.20) | copy-start | bytes 18436
  1020.0 124.3 %all-gather.9.cloned.1.call-start = ((), (), s32[]{:S(2)}) async-start(), calls=%async_computation.6 | async-start | bytes 1310720 | tf_op jit(solution)/shard_map/all_gather | solution.py:115
  1020.9 125.4 %copy-start.1 = (bf16[588,1536]{1,0:T(8,128)(2,1)S(1)}, bf16[588,1536]{1,0:T(8,128)(2,1)}, u32[]{:S(2)}) copy-start(bf16[588,1536]{1,0:T(8,128)(2,1)} %param.12) | copy-start | bytes 5419012
Sparse Core Ops, SparseCore 0:
  49.6 75.9 all-gather.4
  324.4 415.6 reduce-scatter.2
  756.2 220.1 all-gather.6
  1020.1 79.0 reduce-scatter.4
  1119.1 25.2 all-gather.8
